TPU v7x, 32 devices: a whole 2x2x4 slice. The times are simulated.
32 devices in a mesh: shell: 2 (over x), pix: 16 (over z, y, core).
Axes of the slice: x: 2, y: 2, z: 4, core: 2. Of those that a mesh axis runs over, the one named last changes fastest.
Arguments:
- block_tile: int32 [4, 1024], P('shell'), may hold values from 0 to 2047, as said below
- cell_index: int32 [4, 1024, 512], P('shell', 'pix'), may hold values from 0 to 2047
- masses: bfloat16 [4, 1024, 512], P('shell', 'pix'), may hold values from 0.125 to 8, as said below
- plane_coef: float32 [4], P('shell'), may hold values from 0.1 to 0.4
- plane_dist: float32 [4], P('shell'), may hold values from 0.2 to 1
- source_inv: float32 [4], P('shell'), may hold values from 0.5 to 1
Outputs:
- convergence: float32 [4, 2048, 2048], P('shell', 'pix')
- shear_one: float32 [4, 2048, 2048], P('shell', 'pix')
- shear_two: float32 [4, 2048, 2048], P('shell', 'pix')
Inputs may be any that keep to these rules, and one draw needn't show every extreme that they name: `block_tile`: each row is 16 aligned runs of 64 entries, one run per index of pix. The entries of a run are distinct, and at most 8 of them lie in one index's rows of tiles (tile b lies in the rows of index b // 128). In every plane some index receives exactly 8 tiles from every run. `masses`: positive particle weights.
All inputs are finite; a program needn't handle non-finite values.
Results may differ from a plain program's by a relative error of at most 0.0003.
Values sent between devices are 32-bit elements; how exact they have to be, the bound alone decides.
A program may use at most 64 MiB of HBM per device.

v0:
```python
from functools import partial
import math
import jax
import jax.numpy as jnp
from jax import lax
from jax.sharding import PartitionSpec as P

L = 2048
TR = 16
TC = 128
HIGHEST = lax.Precision.HIGHEST


def entering(value, axis, join, neutral):
    count, mine = (lax.axis_size(axis), lax.axis_index(axis))
    pieces = jax.tree.map(lambda part: lax.all_gather(part, axis), value)
    running = jax.tree.map(
        lambda part, zero: jnp.full_like(part, 0) + jnp.asarray(zero, part.dtype), value, neutral
    )

    def lap(position, running):
        longer = join(running, jax.tree.map(lambda part: part[position], pieces))
        return jax.tree.map(lambda new, old: jnp.where(position < mine, new, old), longer, running)

    return lax.fori_loop(0, count - 1, lap, running)


def dft_table(left_size, right_size, period, sign_value):
    left_idx = jnp.arange(left_size)[:, None]
    right_idx = jnp.arange(right_size)[None, :]
    angle = 2.0 * math.pi / period * (left_idx * right_idx % period).astype(jnp.float32)
    return (jnp.cos(angle), sign_value * jnp.sin(angle))


def mix_outer(table, real_part, imag_part):
    cosine, sine_part = table
    contract = partial(jnp.einsum, "ab,...bc->...ac", precision=HIGHEST)
    return (
        contract(cosine, real_part) - contract(sine_part, imag_part),
        contract(sine_part, real_part) + contract(cosine, imag_part),
    )


def mix_inner(table, real_part, imag_part):
    cosine, sine_part = table
    product = partial(jnp.matmul, precision=HIGHEST)
    return (
        product(real_part, cosine) - product(imag_part, sine_part),
        product(real_part, sine_part) + product(imag_part, cosine),
    )


def twist(table, real_part, imag_part):
    cosine, sine_part = table
    return (real_part * cosine - imag_part * sine_part, real_part * sine_part + imag_part * cosine)


def transform_last(real_part, imag_part, sign_value):
    length = real_part.shape[-1]
    inner = math.gcd(length, 128)
    outer = length // inner
    leading = real_part.shape[:-1]
    real_part = real_part.reshape(leading + (outer, inner))
    imag_part = imag_part.reshape(leading + (outer, inner))
    outer_table = dft_table(outer, outer, outer, sign_value)
    inner_table = dft_table(inner, inner, inner, sign_value)
    twiddle = dft_table(outer, inner, length, sign_value)
    if sign_value < 0:
        real_part, imag_part = mix_outer(outer_table, real_part, imag_part)
        real_part, imag_part = twist(twiddle, real_part, imag_part)
        real_part, imag_part = mix_inner(inner_table, real_part, imag_part)
    else:
        real_part, imag_part = mix_inner(inner_table, real_part, imag_part)
        real_part, imag_part = twist(twiddle, real_part, imag_part)
        real_part, imag_part = mix_outer(outer_table, real_part, imag_part)
    return (real_part.reshape(leading + (length,)), imag_part.reshape(leading + (length,)))


def frequency_of(position, length):
    inner = math.gcd(length, 128)
    outer = length // inner
    frequency = position // inner + outer * (position % inner)
    signed = jnp.where(frequency >= length // 2, frequency - length, frequency).astype(jnp.float32)
    keep_mask = (frequency != length // 2).astype(jnp.float32)
    return (signed, keep_mask)


def add_pairs(earlier_pair, later_pair):
    return (earlier_pair[0] + later_pair[0], earlier_pair[1] + later_pair[1])


def deposit_group(item):
    cell_ids, weights = item
    tile_rows = cell_ids // TC
    tile_cols = cell_ids % TC
    row_hot = jnp.where(
        tile_rows[:, None, :] == jnp.arange(TR)[None, :, None],
        weights[:, None, :],
        jnp.zeros((), jnp.bfloat16),
    )
    col_hot = (tile_cols[:, :, None] == jnp.arange(TC)[None, None, :]).astype(jnp.bfloat16)
    return jnp.einsum("grk,gkc->grc", row_hot, col_hot, preferred_element_type=jnp.float32)


def rows_to_sending(packed, groups, slab, cols_own):
    count, fields = (packed.shape[0], packed.shape[1])
    return (
        packed.reshape(count, fields, slab, groups, cols_own)
        .transpose(3, 0, 1, 4, 2)
        .reshape(groups, count, fields, cols_own * slab)
    )


def arrived_to_columns(arrived, groups, slab, cols_own):
    count, fields = (arrived.shape[1], arrived.shape[2])
    return (
        arrived.reshape(groups, count, fields, cols_own, slab)
        .transpose(1, 2, 3, 0, 4)
        .reshape(count, fields, cols_own, groups * slab)
    )


def columns_to_sending(stacked, groups, slab, cols_own):
    count, fields = (stacked.shape[0], stacked.shape[1])
    return (
        stacked.reshape(count, fields, cols_own, groups, slab)
        .transpose(3, 0, 1, 2, 4)
        .reshape(groups, count, fields, cols_own * slab)
    )


def landed_to_rows(landed, groups, slab, cols_own):
    count, fields = (landed.shape[1], landed.shape[2])
    return (
        landed.reshape(groups, count, fields, cols_own, slab)
        .transpose(1, 2, 4, 0, 3)
        .reshape(count, fields, slab, groups * cols_own)
    )


def local(block_tile, cell_index, masses, plane_coef, plane_dist, source_inv):
    groups = lax.axis_size("pix")
    my_index = lax.axis_index("pix")
    planes, local_tiles, per_tile = cell_index.shape
    slab = L // groups
    per_owner = slab // TR * (L // TC)
    cap = max(1, 2 * local_tiles // groups)
    flat = TR * TC
    batch_tiles = 8
    deposited = lax.map(
        deposit_group,
        (cell_index.reshape(-1, batch_tiles, per_tile), masses.reshape(-1, batch_tiles, per_tile)),
    )
    tile_sums = deposited.reshape(planes, local_tiles, flat)
    table = block_tile.reshape(planes, groups, local_tiles)
    owner = table // per_owner
    earlier = jnp.arange(local_tiles)[:, None] < jnp.arange(local_tiles)[None, :]
    same_owner = owner[:, :, :, None] == owner[:, :, None, :]
    rank = jnp.sum(jnp.where(same_owner & earlier[None, None], 1, 0), axis=2)
    slot = owner * cap + rank
    my_slots = lax.dynamic_index_in_dim(slot, my_index, axis=1, keepdims=False)
    slot_grid = jnp.arange(groups)[:, None] * cap + jnp.arange(cap)[None, :]
    send_hot = (my_slots[:, None, None, :] == slot_grid[None, :, :, None]).astype(jnp.float32)
    outgoing = jnp.einsum("pnct,ptf->npcf", send_hot, tile_sums, precision=HIGHEST)
    incoming = lax.all_to_all(outgoing, "pix", split_axis=0, concat_axis=0, tiled=True)
    local_index = table - my_index * per_owner
    is_mine = owner == my_index
    tile_hot = (is_mine[..., None] & (local_index[..., None] == jnp.arange(per_owner))).astype(
        jnp.float32
    )
    slot_hot = (rank[..., None] == jnp.arange(cap)).astype(jnp.float32)
    placing = jnp.einsum("pstl,pstc->plsc", tile_hot, slot_hot, precision=HIGHEST)
    slab_tiles = jnp.einsum("plsc,spcf->plf", placing, incoming, precision=HIGHEST)
    density = (
        slab_tiles.reshape(planes, slab // TR, L // TC, TR, TC)
        .transpose(0, 1, 3, 2, 4)
        .reshape(planes, slab, L)
    )
    total = lax.psum(jnp.sum(density, axis=(1, 2)), "pix")
    contrast = density / (total / (L * L))[:, None, None] - 1.0
    near_local = jnp.cumsum(plane_coef[:, None, None] * contrast, axis=0)
    far_local = jnp.cumsum((plane_coef * plane_dist)[:, None, None] * contrast, axis=0)
    blank = jnp.zeros((slab, L), jnp.float32)
    near_before, far_before = entering(
        (near_local[-1], far_local[-1]), "shell", add_pairs, (blank, blank)
    )
    convergence = near_before + near_local - source_inv[:, None, None] * (far_before + far_local)
    cols_own = L // groups
    wave_x, keep_x = frequency_of(my_index * cols_own + jnp.arange(cols_own), L)
    wave_y, keep_y = frequency_of(jnp.arange(L), L)
    wave_x = wave_x[:, None]
    wave_y = wave_y[None, :]
    both_keep = keep_x[:, None] * keep_y[None, :]
    wave_power = jnp.maximum(wave_x * wave_x + wave_y * wave_y, 1.0)
    kernel_one = both_keep * (wave_x * wave_x - wave_y * wave_y) / wave_power
    kernel_two = both_keep * 2.0 * wave_x * wave_y / wave_power
    scale = 1.0 / (L * L)
    spec_real, spec_imag = transform_last(convergence[0::2], convergence[1::2], -1.0)
    sending = rows_to_sending(jnp.stack([spec_real, spec_imag], axis=1), groups, slab, cols_own)
    arrived = lax.all_to_all(sending, "pix", split_axis=0, concat_axis=0, tiled=True)
    columns = arrived_to_columns(arrived, groups, slab, cols_own)
    row_real, row_imag = transform_last(columns[:, 0], columns[:, 1], -1.0)
    first_real, first_imag = transform_last(row_real * kernel_one, row_imag * kernel_one, 1.0)
    second_real, second_imag = transform_last(row_real * kernel_two, row_imag * kernel_two, 1.0)
    stacked = jnp.stack([first_real, first_imag, second_real, second_imag], axis=1)
    landed = lax.all_to_all(
        columns_to_sending(stacked, groups, slab, cols_own),
        "pix",
        split_axis=0,
        concat_axis=0,
        tiled=True,
    )
    row_layout = landed_to_rows(landed, groups, slab, cols_own)
    even_one, odd_one = transform_last(row_layout[:, 0], row_layout[:, 1], 1.0)
    even_two, odd_two = transform_last(row_layout[:, 2], row_layout[:, 3], 1.0)
    shear_one = jnp.stack([even_one, odd_one], axis=1).reshape(planes, slab, L)
    shear_two = jnp.stack([even_two, odd_two], axis=1).reshape(planes, slab, L)
    return (convergence, shear_one * scale, shear_two * scale)


def solution(mesh):
    placed = (
        P("shell", None),
        P("shell", "pix", None),
        P("shell", "pix", None),
        P("shell"),
        P("shell"),
        P("shell"),
    )
    return jax.shard_map(
        local,
        mesh=mesh,
        in_specs=placed,
        out_specs=(P("shell", "pix", None), P("shell", "pix", None), P("shell", "pix", None)),
        check_vma=False,
    )
```

profile of v0, /device:TPU:1, one launch (start us, length us, event | category | flops | bytes accessed | tf_op | source)
XLA Modules:
  0.0 498.4 jit_solution(13083244063688740668)
XLA Ops:
  8.0 56.0 %while.8 = (s32[]{:T(128)}, f32[16,8,16,128]{3,2,1,0:T(8,128)S(1)}, s32[16,8,512]{2,1,0:T(8,128)}, bf16[16,8,512]{2,1,0:T(8,128)(2,1)}, s32[]{:T(128)}) while((s32[]{:T(128)}, f32[16,8,16,128]{3,2,1,0:T(8,128)S(1)}, s32[16,8,512]{2,1,0:T(8,128)}, bf16[16,8,512]{2,1,0:T(8,128)(2,1)}, s32[]{:T(128)}) %tuple.63), condition=%wide.region_2.3_spmd, body=%wide.region_1.2_spmd.sunk | while | flops 17534976 | bytes 196693 | solution.py:150
  65.7 2.5 copy.183
  68.2 7.3 %all-to-all-start = ((f32[16,2,8,2048]{3,2,1,0:T(8,128)}), f32[16,2,8,2048]{3,2,1,0:T(8,128)S(1)}, u32[]{:S(2)}, u32[]{:S(2)}) async-start(f32[16,2,8,2048]{3,2,1,0:T(8,128)} %copy.183), calls=%async_computation | async-start | bytes 4194304 | tf_op jit(solution)/shard_map/all_to_all | solution.py:165
  76.9 40.2 %all-to-all-done = f32[16,2,8,2048]{3,2,1,0:T(8,128)S(1)} async-done(((f32[16,2,8,2048]{3,2,1,0:T(8,128)}), f32[16,2,8,2048]{3,2,1,0:T(8,128)S(1)}, u32[]{:S(2)}, u32[]{:S(2)}) %all-to-all-start) | async-done | bytes 2097184 | tf_op jit(solution)/shard_map/all_to_all | solution.py:165
  117.1 3.2 bitcast_reduce_fusion
  120.3 33.9 %psum.7 = f32[2]{0:T(128)S(1)} all-reduce(f32[2]{0:T(128)S(1)} %get-tuple-element.117), channel_id=1, replica_groups=mesh['shell'=2,'pix'=16] {'pix'}, use_global_device_ids=true, to_apply=%region_4.5 | all-reduce | flops 2 | bytes 16 | tf_op jit(solution)/shard_map/psum | solution.py:179
  154.2 2.0 copy.236
  156.2 2.0 copy.185
  158.2 1.7 reshape.931
  165.7 31.5 %all-gather.3.cloned.1.call-done = f32[2,128,2048]{2,1,0:T(8,128)} async-done(((f32[1,128,2048]{2,1,0:T(8,128)}), f32[2,128,2048]{2,1,0:T(8,128)}) %all-gather.3.cloned.1.call-update) | async-done | bytes 2097168 | tf_op jit(solution)/shard_map/all_gather | solution.py:16
  198.6 33.9 %all-gather.5.cloned.1.call-done = f32[2,128,2048]{2,1,0:T(8,128)} async-done(((f32[1,128,2048]{2,1,0:T(8,128)}), f32[2,128,2048]{2,1,0:T(8,128)}) %all-gather.5.cloned.1.call-update) | async-done | bytes 2097168 | tf_op jit(solution)/shard_map/all_gather | solution.py:16
  232.5 1.5 fusion.38
  241.3 1.4 fusion.77
  242.7 1.4 fusion.79
  244.2 1.5 fusion.32
  245.7 2.0 fusion.31
  247.9 1.8 copy.190
  249.7 6.4 %all-to-all-start.1 = ((f32[16,1,2,16384]{3,1,2,0:T(1,128)}), f32[16,1,2,16384]{3,1,2,0:T(1,128)S(1)}, u32[]{:S(2)}, u32[]{:S(2)}) async-start(f32[16,1,2,16384]{3,1,2,0:T(1,128)} %bitcast.319), calls=%async_computation.1 | async-start | bytes 4194304 | tf_op jit(solution)/shard_map/all_to_all | solution.py:200
  256.2 41.4 %all-to-all-done.1 = f32[16,1,2,16384]{3,1,2,0:T(1,128)S(1)} async-done(((f32[16,1,2,16384]{3,1,2,0:T(1,128)}), f32[16,1,2,16384]{3,1,2,0:T(1,128)S(1)}, u32[]{:S(2)}, u32[]{:S(2)}) %all-to-all-start.1) | async-done | bytes 2097184 | tf_op jit(solution)/shard_map/all_to_all | solution.py:200
  297.6 1.8 copy.191
  299.4 2.6 fusion.465
  304.7 1.7 copy.235
  308.7 1.4 fusion.71
  310.2 1.4 fusion.73
  311.6 1.4 convolution_subtract_fusion.8
  313.1 1.4 fusion.100
  314.4 1.6 fusion.97
  316.0 1.4 fusion.114
  317.4 1.4 fusion.118
  318.8 1.4 convolution_add_fusion.8
  320.2 1.4 convolution_add_fusion.5
  321.7 1.4 convolution_subtract_fusion.5
  323.1 1.4 convolution_subtract_fusion.7
  324.5 1.9 multiply_add_fusion.3
  326.4 2.0 fusion.65
  328.4 1.6 fusion.67
  330.0 1.6 fusion.59
  331.6 1.6 fusion.61
  333.3 1.6 fusion.28
  334.9 1.6 fusion.27
  336.6 1.6 fusion.26
  338.2 1.8 fusion.25
  341.7 103.1 %all_to_all.15 = f32[16,1,4,16384]{3,1,2,0:T(1,128)S(1)} all-to-all(f32[16,1,4,16384]{3,1,2,0:T(1,128)S(1)} %bitcast.304), channel_id=1, replica_groups=mesh['shell'=2,'pix'=16] {'pix'}, dimensions={0} | all-to-all | bytes 8388608 | tf_op jit(solution)/shard_map/all_to_all | solution.py:206
  445.6 1.9 fusion.91
  447.6 1.9 fusion.108
  449.5 1.9 fusion.94
  451.4 1.9 fusion.111
  453.4 2.0 convolution_subtract_fusion.3
  455.4 2.2 convolution_add_fusion.3
  457.5 2.0 convolution_subtract_fusion.1
  459.5 2.3 multiply_add_fusion
  461.8 1.6 fusion.47
  463.4 1.6 fusion.49
  465.1 1.6 fusion.53
  466.7 1.6 fusion.55
  468.3 2.8 fusion.22
  471.2 2.6 fusion.21
  473.8 2.4 stack_reshape.21
  476.2 2.4 stack_reshape.20
  478.5 2.6 fusion.24
  481.1 2.6 fusion.23
  483.7 2.5 stack_reshape.9
  487.4 1.5 fusion.14
  489.7 1.5 fusion.13
  (138 shorter events, 83.6 us)
Async XLA Ops:
  68.2 48.9 %all-to-all-start = ((f32[16,2,8,2048]{3,2,1,0:T(8,128)}), f32[16,2,8,2048]{3,2,1,0:T(8,128)S(1)}, u32[]{:S(2)}, u32[]{:S(2)}) async-start(f32[16,2,8,2048]{3,2,1,0:T(8,128)} %copy.183), calls=%async_computation | async-start | bytes 4194304 | tf_op jit(solution)/shard_map/all_to_all | solution.py:165
  75.6 121.7 %all-gather.3.cloned.1.call-start = ((), (), s32[]{:S(2)}) async-start(), calls=%async_computation.3 | async-start | bytes 3145728 | tf_op jit(solution)/shard_map/all_gather | solution.py:16
  158.2 1.7 copy-start.10
  160.2 1.3 copy-start
  161.6 1.4 copy-start.12
  162.7 69.9 %all-gather.5.cloned.1.call-start = ((), (), s32[]{:S(2)}) async-start(), calls=%async_computation.4 | async-start | bytes 3145728 | tf_op jit(solution)/shard_map/all_gather | solution.py:16
  163.3 1.3 copy-start.2
  165.7 68.3 %copy-start.1 = (f32[2,128,2048]{2,1,0:T(8,128)S(1)}, f32[2,128,2048]{2,1,0:T(8,128)}, u32[]{:S(2)}) copy-start(f32[2,128,2048]{2,1,0:T(8,128)} %copy-done) | copy-start | bytes 6291460
  165.7 68.3 %copy-start.11 = (f32[2]{0:T(128)S(1)}, f32[2]{0:T(128)}, u32[]{:S(2)}) copy-start(f32[2]{0:T(128)} %param.13) | copy-start | bytes 28
  232.5 1.9 copy-start.3
  235.1 1.3 copy-start.4
  249.7 47.9 %all-to-all-start.1 = ((f32[16,1,2,16384]{3,1,2,0:T(1,128)}), f32[16,1,2,16384]{3,1,2,0:T(1,128)S(1)}, u32[]{:S(2)}, u32[]{:S(2)}) async-start(f32[16,1,2,16384]{3,1,2,0:T(1,128)} %bitcast.319), calls=%async_computation.1 | async-start | bytes 4194304 | tf_op jit(solution)/shard_map/all_to_all | solution.py:200
  481.1 5.1 %copy-start.5 = (f32[1,128,16,128]{3,2,1,0:T(8,128)S(1)}, f32[1,128,16,128]{3,2,1,0:T(8,128)}, u32[]{:S(2)}) copy-start(f32[1,128,16,128]{3,2,1,0:T(8,128)} %fusion.24) | copy-start | bytes 3145732
  483.7 3.7 copy-start.6
  483.7 3.7 copy-start.7
  487.4 1.5 copy-start.8
  487.4 2.3 copy-start.9
Sparse Core Ops, SparseCore 0:
  162.8 34.4 all-gather.2
  199.4 33.0 all-gather.4
where the time goes:
time: 508 us; the launch traced here: 498 us
  waiting for transfers between devices  147 us (29%)
  blocking collectives  137 us (27%)
  matrix products  106 us (21%)
  local copies, waits for them, and re-layouts  47.2 us (9%)
  other arithmetic  31.7 us (6%)
  between operations  15.1 us (3%)
  starting transfers between devices  14 us (3%)
    all_to_all x1, blocking collectives, local(): lax.all_to_all(columns_to_sending(stacked, groups, slab, cols_own), 'pix'...  103 us
    all_gather x2, waiting for transfers between devices, entering(): pieces = jax.tree.map(lambda part: lax.all_gather(part, axis), value)  65.5 us
    all_to_all x1, waiting for transfers between devices, local(): lax.all_to_all(sending, 'pix', split_axis=0, concat_axis=0, tiled=True)  41.4 us
    all_to_all x1, waiting for transfers between devices, local(): lax.all_to_all(outgoing, 'pix', split_axis=0, concat_axis=0, tiled=True)  40.2 us
    psum x1, blocking collectives, local(): total = lax.psum(jnp.sum(density, axis=(1, 2)), 'pix')  33.9 us
    dot_general x16, matrix products, deposit_group(): jnp.einsum('grk,gkc->grc', row_hot, col_hot, preferred_element_type=jnp.f...  21.1 us
    select_n x16, other arithmetic, deposit_group(): tile_cols = cell_ids % TC  11.7 us
    select_n x16, other arithmetic, deposit_group(): tile_rows = cell_ids // TC  11.7 us
  transfers between devices with their start and end apart: 4, of which 4 were waited for; matrix products, arithmetic and copies ran while one was open for 1% of the time, Pallas kernels for 0%

commit v1 on v0

--- a/solution.py
+++ b/solution.py
@@ -9,6 +9,27 @@
 TR = 16
 TC = 128
 HIGHEST = lax.Precision.HIGHEST
+
+
+def try_all_ends_by_axis(xin, dev_axis, dim_i, d_out):
+    item_now, tile_out = (jax.lax.axis_size(dev_axis), jax.lax.axis_index(dev_axis))
+    now = xin.shape[dim_i] // item_now
+    big = list(xin.shape)
+    big[dim_i] = now
+    f_next = big[d_out]
+    big[d_out] = f_next * item_now
+    parts_out = jnp.zeros(big, xin.dtype)
+    for w in range(item_now):
+        p_next = lax.dynamic_slice_in_dim(xin, (tile_out ^ w) * now, now, axis=dim_i)
+        if w:
+            entries = []
+            for ii in range(item_now):
+                entries.append((ii, ii ^ w))
+            p_next = jax.lax.ppermute(p_next, dev_axis, perm=entries)
+        parts_out = lax.dynamic_update_slice_in_dim(
+            parts_out, p_next, (tile_out ^ w) * f_next, axis=d_out
+        )
+    return parts_out
 
 
 def entering(value, axis, join, neutral):
@@ -197,7 +218,7 @@
     scale = 1.0 / (L * L)
     spec_real, spec_imag = transform_last(convergence[0::2], convergence[1::2], -1.0)
     sending = rows_to_sending(jnp.stack([spec_real, spec_imag], axis=1), groups, slab, cols_own)
-    arrived = lax.all_to_all(sending, "pix", split_axis=0, concat_axis=0, tiled=True)
+    arrived = try_all_ends_by_axis(sending, "pix", 0, 0)
     columns = arrived_to_columns(arrived, groups, slab, cols_own)
     row_real, row_imag = transform_last(columns[:, 0], columns[:, 1], -1.0)
     first_real, first_imag = transform_last(row_real * kernel_one, row_imag * kernel_one, 1.0)

time: 508 us -> 541 us (1.065)
  local copies, waits for them, and re-layouts: 47.2 us -> 61.6 us
  starting transfers between devices: 14 us -> 27.8 us
  waiting for transfers between devices: 147 us -> 156 us
  blocking collectives: 137 us -> 131 us
    ppermute x0 -> x15, waiting for transfers between devices: none -> 50.4 us  [try_all_ends_by_axis(): p_next = jax.lax.ppermute(p_next, dev_axis, perm=entries)]
    all_to_all x1 -> x0, waiting for transfers between devices: 41.4 us -> none  [local(): lax.all_to_all(sending, 'pix', split_axis=0, concat_axis=0, tiled=True)]
    ppermute x0 -> x15, starting transfers between devices: none -> 20.2 us  [try_all_ends_by_axis(): p_next = jax.lax.ppermute(p_next, dev_axis, perm=entries)]
    dynamic_update_slice x0 -> x15, local copies, waits for them, and re-layouts: none -> 9.96 us  [try_all_ends_by_axis(): lax.dynamic_update_slice_in_dim(parts_out, p_next, (tile_out ^ w) * f_nex...]
    all_to_all x1 -> x0, starting transfers between devices: 6.38 us -> none  [local(): lax.all_to_all(sending, 'pix', split_axis=0, concat_axis=0, tiled=True)]
    all_to_all x1, blocking collectives: 103 us -> 97.6 us  [local(): lax.all_to_all(columns_to_sending(stacked, groups, slab, cols_own), 'pix'...]
  transfers between devices with their start and end apart: 4 -> 18, of which waited for: 4 -> 13; matrix products, arithmetic and copies ran while one was open for 1% -> 3% of each run, Pallas kernels for 0% -> 0%
where the time goes in v1:
time: 541 us; the launch traced here: 531 us
  waiting for transfers between devices  156 us (29%)
  blocking collectives  131 us (24%)
  matrix products  106 us (20%)
  local copies, waits for them, and re-layouts  61.6 us (11%)
  other arithmetic  33 us (6%)
  starting transfers between devices  27.8 us (5%)
  between operations  15.3 us (3%)
    all_to_all x1, blocking collectives, local(): lax.all_to_all(columns_to_sending(stacked, groups, slab, cols_own), 'pix'...  97.6 us
    all_gather x2, waiting for transfers between devices, entering(): pieces = jax.tree.map(lambda part: lax.all_gather(part, axis), value)  65.3 us
    ppermute x15, waiting for transfers between devices, try_all_ends_by_axis(): p_next = jax.lax.ppermute(p_next, dev_axis, perm=entries)  50.4 us
    all_to_all x1, waiting for transfers between devices, local(): lax.all_to_all(outgoing, 'pix', split_axis=0, concat_axis=0, tiled=True)  40.2 us
    psum x1, blocking collectives, local(): total = lax.psum(jnp.sum(density, axis=(1, 2)), 'pix')  33.9 us
    dot_general x16, matrix products, deposit_group(): jnp.einsum('grk,gkc->grc', row_hot, col_hot, preferred_element_type=jnp.f...  21.1 us
    ppermute x15, starting transfers between devices, try_all_ends_by_axis(): p_next = jax.lax.ppermute(p_next, dev_axis, perm=entries)  20.2 us
    select_n x16, other arithmetic, deposit_group(): tile_cols = cell_ids % TC  11.7 us
  transfers between devices with their start and end apart: 18, of which 13 were waited for; matrix products, arithmetic and copies ran while one was open for 3% of the time, Pallas kernels for 0%

profile of v1, /device:TPU:1, one launch (start us, length us, event | category | flops | bytes accessed | tf_op | source)
XLA Modules:
  0.0 531.2 jit_solution(5946017822149868616)
XLA Ops:
  8.0 56.0 %while.8 = (s32[]{:T(128)}, f32[16,8,16,128]{3,2,1,0:T(8,128)S(1)}, s32[16,8,512]{2,1,0:T(8,128)}, bf16[16,8,512]{2,1,0:T(8,128)(2,1)}, s32[]{:T(128)}) while((s32[]{:T(128)}, f32[16,8,16,128]{3,2,1,0:T(8,128)S(1)}, s32[16,8,512]{2,1,0:T(8,128)}, bf16[16,8,512]{2,1,0:T(8,128)(2,1)}, s32[]{:T(128)}) %tuple.78), condition=%wide.region_2.3_spmd, body=%wide.region_1.2_spmd.sunk | while | flops 17534976 | bytes 196693 | solution.py:171
  65.7 2.5 copy.183
  68.2 7.3 %all-to-all-start = ((f32[16,2,8,2048]{3,2,1,0:T(8,128)}), f32[16,2,8,2048]{3,2,1,0:T(8,128)S(1)}, u32[]{:S(2)}, u32[]{:S(2)}) async-start(f32[16,2,8,2048]{3,2,1,0:T(8,128)} %copy.183), calls=%async_computation | async-start | bytes 4194304 | tf_op jit(solution)/shard_map/all_to_all | solution.py:186
  76.9 40.2 %all-to-all-done = f32[16,2,8,2048]{3,2,1,0:T(8,128)S(1)} async-done(((f32[16,2,8,2048]{3,2,1,0:T(8,128)}), f32[16,2,8,2048]{3,2,1,0:T(8,128)S(1)}, u32[]{:S(2)}, u32[]{:S(2)}) %all-to-all-start) | async-done | bytes 2097184 | tf_op jit(solution)/shard_map/all_to_all | solution.py:186
  117.1 3.2 bitcast_reduce_fusion
  120.3 33.9 %psum.7 = f32[2]{0:T(128)S(1)} all-reduce(f32[2]{0:T(128)S(1)} %get-tuple-element.133), channel_id=1, replica_groups=mesh['shell'=2,'pix'=16] {'pix'}, use_global_device_ids=true, to_apply=%region_4.5 | all-reduce | flops 2 | bytes 16 | tf_op jit(solution)/shard_map/psum | solution.py:200
  154.2 2.0 copy.236
  156.2 2.0 copy.185
  158.2 1.7 reshape.931
  166.0 31.4 %all-gather.3.cloned.1.call-done = f32[2,128,2048]{2,1,0:T(8,128)} async-done(((f32[1,128,2048]{2,1,0:T(8,128)}), f32[2,128,2048]{2,1,0:T(8,128)}) %all-gather.3.cloned.1.call-update) | async-done | bytes 2097168 | tf_op jit(solution)/shard_map/all_gather | solution.py:37
  198.6 33.9 %all-gather.5.cloned.1.call-done = f32[2,128,2048]{2,1,0:T(8,128)} async-done(((f32[1,128,2048]{2,1,0:T(8,128)}), f32[2,128,2048]{2,1,0:T(8,128)}) %all-gather.5.cloned.1.call-update) | async-done | bytes 2097168 | tf_op jit(solution)/shard_map/all_gather | solution.py:37
  244.2 1.5 fusion.32
  245.7 1.9 fusion.31
  249.1 1.9 copy.190
  251.0 3.3 broadcast_in_dim.53
  254.3 2.5 constant_dynamic-slice_fusion
  257.6 3.9 collective-permute-start.14
  261.8 3.7 collective-permute-start.12
  267.5 5.1 collective-permute-done.1
  274.0 4.2 collective-permute-done.2
  278.9 4.0 collective-permute-done.3
  284.7 3.7 collective-permute-done.4
  290.2 2.9 collective-permute-done.5
  293.2 3.1 collective-permute-start.6
  296.9 2.7 collective-permute-done.6
  299.7 2.8 collective-permute-start.7
  303.1 5.2 collective-permute-done.7
  309.9 7.5 %collective-permute-done.8 = f32[1,1,2,16384]{3,1,2,0:T(1,128)S(1)} collective-permute-done((f32[1,1,2,16384]{3,1,2,0:T(1,128)S(1)}, f32[1,1,2,16384]{3,1,2,0:T(1,128)S(1)}, u32[]{:S(2)}, u32[]{:S(2)}) %collective-permute-start.8) | collective-permute-done | bytes 131104 | tf_op jit(solution)/shard_map/ppermute | solution.py:28
  318.3 8.0 %collective-permute-done.9 = f32[1,1,2,16384]{3,1,2,0:T(1,128)S(1)} collective-permute-done((f32[1,1,2,16384]{3,1,2,0:T(1,128)S(1)}, f32[1,1,2,16384]{3,1,2,0:T(1,128)S(1)}, u32[]{:S(2)}, u32[]{:S(2)}) %collective-permute-start.9) | collective-permute-done | bytes 131104 | tf_op jit(solution)/shard_map/ppermute | solution.py:28
  327.0 7.0 %collective-permute-done.10 = f32[1,1,2,16384]{3,1,2,0:T(1,128)S(1)} collective-permute-done((f32[1,1,2,16384]{3,1,2,0:T(1,128)S(1)}, f32[1,1,2,16384]{3,1,2,0:T(1,128)S(1)}, u32[]{:S(2)}, u32[]{:S(2)}) %collective-permute-start.10) | collective-permute-done | bytes 131104 | tf_op jit(solution)/shard_map/ppermute | solution.py:28
  337.3 1.9 copy.191
  343.0 1.7 copy.235
  352.8 1.6 fusion.97
  362.9 1.9 multiply_add_fusion.3
  364.7 2.0 fusion.65
  366.7 1.6 fusion.67
  368.4 1.6 fusion.59
  370.0 1.6 fusion.61
  371.6 1.6 fusion.28
  373.3 1.6 fusion.27
  374.9 1.6 fusion.26
  376.5 1.8 fusion.25
  380.1 97.6 %all_to_all.10 = f32[16,1,4,16384]{3,1,2,0:T(1,128)S(1)} all-to-all(f32[16,1,4,16384]{3,1,2,0:T(1,128)S(1)} %bitcast.304), channel_id=1, replica_groups=mesh['shell'=2,'pix'=16] {'pix'}, dimensions={0} | all-to-all | bytes 8388608 | tf_op jit(solution)/shard_map/all_to_all | solution.py:227
  478.4 1.9 fusion.91
  480.4 1.9 fusion.108
  482.3 1.9 fusion.94
  484.3 1.9 fusion.111
  486.2 2.0 convolution_subtract_fusion.3
  488.2 2.2 convolution_add_fusion.3
  490.4 2.0 convolution_subtract_fusion.1
  492.3 2.3 multiply_add_fusion
  494.6 1.6 fusion.47
  496.3 1.6 fusion.49
  497.9 1.6 fusion.53
  499.5 1.6 fusion.55
  501.2 2.8 fusion.22
  504.0 2.6 fusion.21
  506.6 2.4 stack_reshape.21
  509.0 2.3 stack_reshape.20
  511.3 2.6 fusion.24
  513.9 2.6 fusion.23
  516.5 2.5 stack_reshape.9
  520.2 1.5 fusion.14
  522.5 1.5 fusion.13
  (183 shorter events, 121.1 us)
Async XLA Ops:
  68.2 48.9 %all-to-all-start = ((f32[16,2,8,2048]{3,2,1,0:T(8,128)}), f32[16,2,8,2048]{3,2,1,0:T(8,128)S(1)}, u32[]{:S(2)}, u32[]{:S(2)}) async-start(f32[16,2,8,2048]{3,2,1,0:T(8,128)} %copy.183), calls=%async_computation | async-start | bytes 4194304 | tf_op jit(solution)/shard_map/all_to_all | solution.py:186
  75.6 121.7 %all-gather.3.cloned.1.call-start = ((), (), s32[]{:S(2)}) async-start(), calls=%async_computation.2 | async-start | bytes 3145728 | tf_op jit(solution)/shard_map/all_gather | solution.py:37
  158.2 1.7 copy-start.10
  160.2 1.3 copy-start
  161.6 1.4 copy-start.12
  162.7 69.9 %all-gather.5.cloned.1.call-start = ((), (), s32[]{:S(2)}) async-start(), calls=%async_computation.3 | async-start | bytes 3145728 | tf_op jit(solution)/shard_map/all_gather | solution.py:37
  163.3 1.3 copy-start.2
  165.9 68.1 %copy-start.1 = (f32[2,128,2048]{2,1,0:T(8,128)S(1)}, f32[2,128,2048]{2,1,0:T(8,128)}, u32[]{:S(2)}) copy-start(f32[2,128,2048]{2,1,0:T(8,128)} %copy-done) | copy-start | bytes 6291460
  165.9 68.1 %copy-start.11 = (f32[2]{0:T(128)S(1)}, f32[2]{0:T(128)}, u32[]{:S(2)}) copy-start(f32[2]{0:T(128)} %param.13) | copy-start | bytes 28
  232.6 1.9 copy-start.3
  235.2 1.3 copy-start.4
  256.8 8.9 %collective-permute-start = (f32[1,1,2,16384]{3,1,2,0:T(1,128)S(1)}, f32[1,1,2,16384]{3,1,2,0:T(1,128)S(1)}, u32[]{:S(2)}, u32[]{:S(2)}) collective-permute-start(f32[1,1,2,16384]{3,1,2,0:T(1,128)S(1)} %get-tuple-element.125), channel_id=1, source_target_pairs={{0,1},{1,0},{2,3},{3,2},{4,5},{5,4},{6,7},{7,6},{8,9},{9,8},{10,11... | collective-permute-start | bytes 393224 | tf_op jit(solution)/shard_map/ppermute | solution.py:28
  257.6 79.0 %collective-permute-start.14 = (f32[1,1,2,16384]{3,1,2,0:T(1,128)S(1)}, f32[1,1,2,16384]{3,1,2,0:T(1,128)S(1)}, u32[]{:S(2)}, u32[]{:S(2)}) collective-permute-start(f32[1,1,2,16384]{3,1,2,0:T(1,128)S(1)} %get-tuple-element.111), channel_id=1, source_target_pairs={{0,15},{1,14},{2,13},{3,12},{4,11},{5,10},{6,9},{7,8},{8,7},{9,6},... | collective-permute-start | bytes 393224 | tf_op jit(solution)/shard_map/ppermute | solution.py:28
  261.6 74.4 %collective-permute-start.13 = (f32[1,1,2,16384]{3,1,2,0:T(1,128)S(1)}, f32[1,1,2,16384]{3,1,2,0:T(1,128)S(1)}, u32[]{:S(2)}, u32[]{:S(2)}) collective-permute-start(f32[1,1,2,16384]{3,1,2,0:T(1,128)S(1)} %get-tuple-element.112), channel_id=1, source_target_pairs={{0,14},{1,15},{2,12},{3,13},{4,10},{5,11},{6,8},{7,9},{8,6},{9,7},... | collective-permute-start | bytes 393224 | tf_op jit(solution)/shard_map/ppermute | solution.py:28
  261.8 73.6 %collective-permute-start.12 = (f32[1,1,2,16384]{3,1,2,0:T(1,128)S(1)}, f32[1,1,2,16384]{3,1,2,0:T(1,128)S(1)}, u32[]{:S(2)}, u32[]{:S(2)}) collective-permute-start(f32[1,1,2,16384]{3,1,2,0:T(1,128)S(1)} %get-tuple-element.113), channel_id=1, source_target_pairs={{0,13},{1,12},{2,15},{3,14},{4,9},{5,8},{6,11},{7,10},{8,5},{9,4},... | collective-permute-start | bytes 393224 | tf_op jit(solution)/shard_map/ppermute | solution.py:28
  265.5 69.2 %collective-permute-start.11 = (f32[1,1,2,16384]{3,1,2,0:T(1,128)S(1)}, f32[1,1,2,16384]{3,1,2,0:T(1,128)S(1)}, u32[]{:S(2)}, u32[]{:S(2)}) collective-permute-start(f32[1,1,2,16384]{3,1,2,0:T(1,128)S(1)} %get-tuple-element.114), channel_id=1, source_target_pairs={{0,12},{1,13},{2,14},{3,15},{4,8},{5,9},{6,10},{7,11},{8,4},{9,5},... | collective-permute-start | bytes 393224 | tf_op jit(solution)/shard_map/ppermute | solution.py:28
  265.7 6.9 %collective-permute-start.1 = (f32[1,1,2,16384]{3,1,2,0:T(1,128)S(1)}, f32[1,1,2,16384]{3,1,2,0:T(1,128)S(1)}, u32[]{:S(2)}, u32[]{:S(2)}) collective-permute-start(f32[1,1,2,16384]{3,1,2,0:T(1,128)S(1)} %get-tuple-element.124), channel_id=1, source_target_pairs={{0,2},{1,3},{2,0},{3,1},{4,6},{5,7},{6,4},{7,5},{8,10},{9,11},{10,... | collective-permute-start | bytes 393224 | tf_op jit(solution)/shard_map/ppermute | solution.py:28
  272.6 5.6 %collective-permute-start.2 = (f32[1,1,2,16384]{3,1,2,0:T(1,128)S(1)}, f32[1,1,2,16384]{3,1,2,0:T(1,128)S(1)}, u32[]{:S(2)}, u32[]{:S(2)}) collective-permute-start(f32[1,1,2,16384]{3,1,2,0:T(1,128)S(1)} %get-tuple-element.123), channel_id=1, source_target_pairs={{0,3},{1,2},{2,1},{3,0},{4,7},{5,6},{6,5},{7,4},{8,11},{9,10},{10,... | collective-permute-start | bytes 393224 | tf_op jit(solution)/shard_map/ppermute | solution.py:28
  278.2 4.7 collective-permute-start.3
  282.9 5.5 %collective-permute-start.4 = (f32[1,1,2,16384]{3,1,2,0:T(1,128)S(1)}, f32[1,1,2,16384]{3,1,2,0:T(1,128)S(1)}, u32[]{:S(2)}, u32[]{:S(2)}) collective-permute-start(f32[1,1,2,16384]{3,1,2,0:T(1,128)S(1)} %get-tuple-element.121), channel_id=1, source_target_pairs={{0,5},{1,4},{2,7},{3,6},{4,1},{5,0},{6,3},{7,2},{8,13},{9,12},{10,... | collective-permute-start | bytes 393224 | tf_op jit(solution)/shard_map/ppermute | solution.py:28
  288.4 4.7 collective-permute-start.5
  293.2 6.5 %collective-permute-start.6 = (f32[1,1,2,16384]{3,1,2,0:T(1,128)S(1)}, f32[1,1,2,16384]{3,1,2,0:T(1,128)S(1)}, u32[]{:S(2)}, u32[]{:S(2)}) collective-permute-start(f32[1,1,2,16384]{3,1,2,0:T(1,128)S(1)} %get-tuple-element.119), channel_id=1, source_target_pairs={{0,7},{1,6},{2,5},{3,4},{4,3},{5,2},{6,1},{7,0},{8,15},{9,14},{10,... | collective-permute-start | bytes 393224 | tf_op jit(solution)/shard_map/ppermute | solution.py:28
  299.7 8.7 %collective-permute-start.7 = (f32[1,1,2,16384]{3,1,2,0:T(1,128)S(1)}, f32[1,1,2,16384]{3,1,2,0:T(1,128)S(1)}, u32[]{:S(2)}, u32[]{:S(2)}) collective-permute-start(f32[1,1,2,16384]{3,1,2,0:T(1,128)S(1)} %get-tuple-element.118), channel_id=1, source_target_pairs={{0,8},{1,9},{2,10},{3,11},{4,12},{5,13},{6,14},{7,15},{8,0},{9,1},... | collective-permute-start | bytes 393224 | tf_op jit(solution)/shard_map/ppermute | solution.py:28
  308.3 9.1 %collective-permute-start.8 = (f32[1,1,2,16384]{3,1,2,0:T(1,128)S(1)}, f32[1,1,2,16384]{3,1,2,0:T(1,128)S(1)}, u32[]{:S(2)}, u32[]{:S(2)}) collective-permute-start(f32[1,1,2,16384]{3,1,2,0:T(1,128)S(1)} %get-tuple-element.117), channel_id=1, source_target_pairs={{0,9},{1,8},{2,11},{3,10},{4,13},{5,12},{6,15},{7,14},{8,1},{9,0},... | collective-permute-start | bytes 393224 | tf_op jit(solution)/shard_map/ppermute | solution.py:28
  317.4 8.9 %collective-permute-start.9 = (f32[1,1,2,16384]{3,1,2,0:T(1,128)S(1)}, f32[1,1,2,16384]{3,1,2,0:T(1,128)S(1)}, u32[]{:S(2)}, u32[]{:S(2)}) collective-permute-start(f32[1,1,2,16384]{3,1,2,0:T(1,128)S(1)} %get-tuple-element.116), channel_id=1, source_target_pairs={{0,10},{1,11},{2,8},{3,9},{4,14},{5,15},{6,12},{7,13},{8,2},{9,3},... | collective-permute-start | bytes 393224 | tf_op jit(solution)/shard_map/ppermute | solution.py:28
  326.3 7.7 %collective-permute-start.10 = (f32[1,1,2,16384]{3,1,2,0:T(1,128)S(1)}, f32[1,1,2,16384]{3,1,2,0:T(1,128)S(1)}, u32[]{:S(2)}, u32[]{:S(2)}) collective-permute-start(f32[1,1,2,16384]{3,1,2,0:T(1,128)S(1)} %get-tuple-element.115), channel_id=1, source_target_pairs={{0,11},{1,10},{2,9},{3,8},{4,15},{5,14},{6,13},{7,12},{8,3},{9,2},... | collective-permute-start | bytes 393224 | tf_op jit(solution)/shard_map/ppermute | solution.py:28
  513.9 5.1 copy-start.5
  516.5 3.7 copy-start.6
  516.5 3.7 copy-start.7
  520.2 1.5 copy-start.8
  520.2 2.3 copy-start.9
Sparse Core Ops, SparseCore 0:
  162.8 34.4 all-gather.2
  199.4 33.0 all-gather.4
